TPU v7x, 128 devices: a whole 4x4x4 slice. The times are simulated.
128 devices in a mesh: seq: 16 (over x_lo, z, core), head: 4 (over y), batch: 2 (over x_hi).
Axes of the slice: x: 4 (x_hi: 2, x_lo: 2; x = x_hi * 2 + x_lo), y: 4, z: 4, core: 2. Of those that a mesh axis runs over, the one named last changes fastest.
Arguments:
- tokens: bfloat16 [32768, 2048], P(('batch', 'seq')), parts along dimension 0, may hold values from -6 to 6
- neighbor_bank: bfloat16 [512, 256, 2048], P(('batch', 'seq')), parts along dimension 0, may hold values from -2100 to 2100
- slots: int32 [512], P(('batch', 'seq')), parts along dimension 0, may hold values from 0 to 15
- w_query: bfloat16 [2048, 2048], P('seq', 'head'), may hold values from -0.125 to 0.125
- w_key: bfloat16 [2048, 2048], P('seq', 'head'), may hold values from -0.125 to 0.125
- w_value: bfloat16 [2048, 2048], P('seq', 'head'), may hold values from -0.125 to 0.125
- w_out: bfloat16 [2048, 2048], P('head', 'seq'), may hold values from -0.125 to 0.125
Outputs:
- cross_out: bfloat16 [32768, 2048], P(('batch', 'seq'), 'head'), parts along dimension 0
There are 2 independent parts, one for each index of `batch`. A program takes and returns all parts, laid end to end along the dimension named above; an argument that names none is the same for every part. Nothing has to cross between parts.
Inputs may be any that keep to these rules, and one draw needn't show every extreme that they name: Entry c picks row c // 16 * 16 + slots[c] of neighbor_bank.
All inputs are finite; a program needn't handle non-finite values.
Results may differ from a plain program's by a relative error of at most 0.006.
The roundings to bfloat16 on the way count: a program that leaves them out, or rounds other values in their place, can miss the bound.
Values may be sent and summed in bfloat16 or wider, within the bound.
No kernel may reach another device: no remote copies, remote signals or barrier semaphores. Data moves between devices by JAX's collectives and lax.ppermute only.
A program may use at most 128 MiB of HBM per device.

v0:
```python
import math
import jax
import jax.numpy as jnp
from jax import lax
from jax.sharding import PartitionSpec as P

HEAD_DIM = 128


def passed_along(block, axis, distance):
    devices = range(lax.axis_size(axis))
    route = [(i - distance, i) for i in devices if i - distance in devices]
    return lax.ppermute(block, axis, route)


def side_by_side(arrays, axis, dim, along):
    ends, at = ([], 0)
    for a in arrays[:-1]:
        at += a.shape[along]
        ends.append(at)
    both = jnp.concatenate(arrays, axis=along)
    return tuple(jnp.split(lax.all_gather(both, axis, axis=dim, tiled=True), ends, axis=along))


def attend(query_blocks, key_blocks, value_blocks):
    scores = jnp.einsum(
        "cmhd,cnhd->chmn", query_blocks, key_blocks, preferred_element_type=jnp.float32
    ) / math.sqrt(HEAD_DIM)
    peak_score = jnp.max(scores, axis=-1, keepdims=True)
    exponent = jnp.exp(scores - peak_score)
    weights = (exponent / jnp.sum(exponent, axis=-1, keepdims=True)).astype(jnp.bfloat16)
    blended = jnp.einsum(
        "chmn,cnhd->cmhd", weights, value_blocks, preferred_element_type=jnp.float32
    ).astype(jnp.bfloat16)
    return blended.reshape(blended.shape[0] * blended.shape[1], blended.shape[2] * blended.shape[3])


def fold_rows(source, shard_rows):
    return jnp.dot(source, shard_rows, preferred_element_type=jnp.float32)


def local(tokens, neighbor_bank, slots, w_query, w_key, w_value, w_out):
    tok_rows, model_width = tokens.shape
    block_count = neighbor_bank.shape[0]
    neighbor_rows = neighbor_bank.shape[1]
    block_len = tok_rows // block_count
    local_width = w_query.shape[1]
    local_heads = local_width // HEAD_DIM
    hidden = tokens.astype(jnp.float32)
    normed = (hidden * lax.rsqrt(jnp.mean(hidden * hidden, axis=-1, keepdims=True) + 1e-06)).astype(
        jnp.bfloat16
    )
    retrieved = jnp.take(neighbor_bank, slots, axis=0)
    arrived = passed_along(retrieved[block_count - 1], "seq", 1)
    context = jnp.concatenate([arrived[None], retrieved[: block_count - 1]], axis=0)
    context_flat = context.reshape(block_count * neighbor_rows, model_width)
    shard_rows = side_by_side((w_query, w_key, w_value), "seq", 0, 1)
    query_sum = fold_rows(normed, shard_rows[0])
    key_sum = fold_rows(context_flat, shard_rows[1])
    value_sum = fold_rows(context_flat, shard_rows[2])
    query_blocks = query_sum.astype(jnp.bfloat16).reshape(
        block_count, block_len, local_heads, HEAD_DIM
    )
    key_blocks = key_sum.astype(jnp.bfloat16).reshape(
        block_count, neighbor_rows, local_heads, HEAD_DIM
    )
    value_blocks = value_sum.astype(jnp.bfloat16).reshape(
        block_count, neighbor_rows, local_heads, HEAD_DIM
    )
    attended = attend(query_blocks, key_blocks, value_blocks)
    every_head = lax.all_gather(attended, "head", axis=1, tiled=True)
    wide_rows = lax.all_gather(w_out, "seq", axis=1, tiled=True)
    own_columns = lax.all_to_all(wide_rows, "head", split_axis=1, concat_axis=0, tiled=True)
    return jnp.dot(every_head, own_columns, preferred_element_type=jnp.float32).astype(jnp.bfloat16)


def solution(mesh):
    in_specs = (
        P(("batch", "seq"), None),
        P(("batch", "seq"), None, None),
        P(("batch", "seq")),
        P("seq", "head"),
        P("seq", "head"),
        P("seq", "head"),
        P("head", "seq"),
    )
    out_specs = P(("batch", "seq"), "head")
    return jax.shard_map(local, mesh=mesh, in_specs=in_specs, out_specs=out_specs, check_vma=False)
```

profile of v0, /device:TPU:3, one launch (start us, length us, event | category | flops | bytes accessed | tf_op | source)
XLA Modules:
  0.0 214.9 jit_solution(9233872285534013376)
XLA Ops:
  6.5 0.0 all-gather.4.cloned.1.call-start
  6.5 1.8 pad_maximum_fusion.1
  8.3 0.0 all-gather.4.cloned.1.call-update
  8.4 0.0 all-gather.8.cloned.1.call-start
  8.4 0.7 compare_select_fusion
  9.1 0.0 copy-start.4
  9.1 13.1 %gather_fusion = bf16[16,256,2048]{2,1,0:T(8,128)(2,1)} fusion(bf16[16,256,2048]{2,1,0:T(8,128)(2,1)} %param.8, s32[1024]{0:T(1024)S(1)} %pad_clamp_fusion), kind=kCustom, calls=%fused_computation | custom fusion | bytes 33554496 | tf_op jit(solution)/shard_map/jit(_take)/gather | solution.py:53
  22.2 0.0 copy-done.4
  22.2 0.0 copy-start.3
  22.2 8.7 %broadcast_select_fusion = bf16[16,256,2048]{2,1,0:T(8,128)(2,1)S(1)} fusion(bf16[16,256,2048]{2,1,0:T(8,128)(2,1)} %gather_fusion, pred[16]{0:T(512)(128)(4,1)S(1)} %compare_and_fusion), kind=kLoop, calls=%fused_computation.3 | loop fusion | flops 8388608 | bytes 33554448 | tf_op jit(solution)/shard_map/jit(_take)/select_n | solution.py:53
  31.0 0.0 copy-start
  31.0 5.9 %copy-done = bf16[16,256,2048]{2,1,0:T(8,128)(2,1)} copy-done((bf16[16,256,2048]{2,1,0:T(8,128)(2,1)}, bf16[16,256,2048]{2,1,0:T(8,128)(2,1)S(1)}, u32[]{:S(2)}) %copy-start) | copy-done | bytes 16777240
  36.9 0.1 slice_bitcast_fusion
  37.0 4.1 %collective-permute-start = (bf16[256,2048]{1,0:T(8,128)(2,1)S(1)}, bf16[256,2048]{1,0:T(8,128)(2,1)S(1)}, u32[]{:S(2)}, u32[]{:S(2)}) collective-permute-start(bf16[256,2048]{1,0:T(8,128)(2,1)S(1)} %slice_bitcast_fusion), channel_id=1, source_target_pairs={{0,8},{8,16},{16,24},{24,32},{32,40},{40,48},{48,56},{56,64},{64,7... | collective-permute-start | bytes 3145736 | tf_op jit(solution)/shard_map/ppermute | solution.py:13
  41.1 0.0 copy-done.3
  41.1 0.8 copy.19
  41.9 0.0 all-gather.8.cloned.1.call-update
  41.9 0.0 all-gather.6.cloned.1.call-start
  42.0 0.0 copy-start.1
  42.0 0.0 slice-start
  42.0 2.2 %copy-done.1 = bf16[1024,2048]{1,0:T(8,128)(2,1)S(1)} copy-done((bf16[1024,2048]{1,0:T(8,128)(2,1)S(1)}, bf16[1024,2048]{1,0:T(8,128)(2,1)}, u32[]{:S(2)}) %copy-start.1) | copy-done | bytes 4194328
  44.2 0.9 fusion.1
  45.1 16.4 %collective-permute-done = bf16[256,2048]{1,0:T(8,128)(2,1)S(1)} collective-permute-done((bf16[256,2048]{1,0:T(8,128)(2,1)S(1)}, bf16[256,2048]{1,0:T(8,128)(2,1)S(1)}, u32[]{:S(2)}, u32[]{:S(2)}) %collective-permute-start) | collective-permute-done | bytes 1048608 | tf_op jit(solution)/shard_map/ppermute | solution.py:13
  61.5 0.0 slice-done
  61.5 6.4 %pad_maximum_fusion = bf16[16,256,2048]{2,1,0:T(8,128)(2,1)} fusion(bf16[15,256,2048]{2,1,0:T(8,128)(2,1)S(1)} %slice-done, bf16[1,256,2048]{2,1,0:T(8,128)(2,1)S(1)} %bitcast.25), kind=kLoop, calls=%fused_computation.2 | loop fusion | flops 8388608 | bytes 33554432 | tf_op jit(solution)/shard_map/concatenate | solution.py:55
  68.0 0.0 all-gather.4.cloned.1.call-done
  68.0 14.5 %convolution_convert_fusion = bf16[4096,512]{1,0:T(8,128)(2,1)} fusion(bf16[4096,2048]{1,0:T(8,128)(2,1)} %bitcast.18, bf16[2048,1536]{1,0:T(8,128)(2,1)} %all-gather.4.cloned.1.call-done), kind=kOutput, calls=%fused_computation.8 | convolution fusion | flops 8592031744 | bytes 23068672 | tf_op jit(solution)/shard_map/dot_general | solution.py:39
  82.4 7.0 %reshape.36 = bf16[16,256,4,128]{3,2,1,0:T(4,128)(2,1)} reshape(bf16[4096,512]{1,0:T(8,128)(2,1)} %convolution_convert_fusion) | data formatting | bytes 8388608 | tf_op jit(solution)/shard_map/reshape | solution.py:64
  89.4 5.2 %fusion.21 = bf16[1024,512]{1,0:T(8,128)(2,1)S(1)} fusion(bf16[2048,1536]{1,0:T(8,128)(2,1)} %all-gather.4.cloned.1.call-done, bf16[1024,2048]{1,0:T(8,128)(2,1)} %param.7, f32[1024]{0:T(1024)S(1)} %add_rsqrt_fusion), kind=kOutput, calls=%fused_computation.26 | convolution fusion | flops 2154299392 | bytes 7344128 | tf_op jit(solution)/shard_map/dot_general | solution.py:39
  94.6 0.3 reshape.35
  94.9 14.4 %convolution_convert_fusion.1 = bf16[4096,512]{1,0:T(8,128)(2,1)} fusion(bf16[4096,2048]{1,0:T(8,128)(2,1)} %bitcast.19, bf16[2048,1536]{1,0:T(8,128)(2,1)} %all-gather.4.cloned.1.call-done), kind=kOutput, calls=%fused_computation.9 | convolution fusion | flops 8592031744 | bytes 23068672 | tf_op jit(solution)/shard_map/dot_general | solution.py:39
  109.3 6.9 %reshape.34 = bf16[16,256,4,128]{3,2,1,0:T(4,128)(2,1)} reshape(bf16[4096,512]{1,0:T(8,128)(2,1)} %convolution_convert_fusion.1) | data formatting | bytes 8388608 | tf_op jit(solution)/shard_map/reshape | solution.py:67
  116.2 3.8 %fusion.7 = f32[16,4,64,256]{3,2,1,0:T(8,128)S(1)} fusion(bf16[16,256,4,128]{3,2,1,0:T(4,128)(2,1)} %reshape.36, bf16[16,64,4,128]{3,2,1,0:T(4,128)(2,1)S(1)} %reshape.35), kind=kOutput, calls=%fused_computation.13 | convolution fusion | flops 268435456 | bytes 9437184 | tf_op jit(solution)/shard_map/cmhd,cnhd->chmn/dot_general | solution.py:26
  120.0 0.0 copy-start.2
  120.0 2.0 copy-done.2
  122.0 1.6 fusion.38
  123.6 11.9 %fusion.26 = bf16[16,64,4,128]{3,1,2,0:T(8,128)(2,1)S(1)} fusion(bf16[16,256,4,128]{3,2,1,0:T(4,128)(2,1)} %reshape.34, f32[16,4,64]{2,1,0:T(4,128)S(1)} %fusion.38, f32[16,4,64,256]{3,2,1,0:T(8,128)} %copy-done.2), kind=kOutput, calls=%fused_computation.28 | convolution fusion | flops 274206976 | bytes 9453568 | tf_op jit(solution)/shard_map/chmn,cnhd->cmhd/dot_general | solution.py:32
  135.5 0.9 copy.18
  136.4 1.2 copy.33
  137.6 0.0 all-gather.6.cloned.1.call-update
  137.6 0.0 all-gather.8.cloned.1.call-done
  137.6 35.9 %all_to_all.19 = bf16[512,4,512]{0,2,1:T(8,128)(2,1)S(1)} all-to-all(bf16[512,4,512]{0,2,1:T(8,128)(2,1)} %bitcast.23), channel_id=1, replica_groups=mesh['seq'=16,'head'=4,'batch'=2] {'head'}, dimensions={1} | all-to-all | bytes 4194304 | tf_op jit(solution)/shard_map/all_to_all | solution.py:73
  173.5 2.4 %copy.20 = bf16[4,512,512]{2,1,0:T(8,128)(2,1)} copy(bf16[4,512,512]{1,2,0:T(8,128)(2,1)S(1)} %bitcast.20) | data formatting | bytes 4194304 | tf_op jit(solution)/shard_map/all_to_all | solution.py:73
  175.9 26.3 %all-gather.6.cloned.1.call-done = bf16[1024,2048]{1,0:T(8,128)(2,1)} async-done(((bf16[1024,512]{1,0:T(8,128)(2,1)}), bf16[1024,2048]{1,0:T(8,128)(2,1)}) %all-gather.6.cloned.1.call-update) | async-done | bytes 4194320 | tf_op jit(solution)/shard_map/all_gather | solution.py:71
  202.2 6.2 %convolution_convert_fusion.2 = bf16[1024,512]{1,0:T(8,128)(2,1)} fusion(bf16[1024,2048]{1,0:T(8,128)(2,1)} %all-gather.6.cloned.1.call-done, bf16[2048,512]{1,0:T(8,128)(2,1)} %bitcast.24), kind=kOutput, calls=%fused_computation.27 | convolution fusion | flops 2148007936 | bytes 7340032 | tf_op jit(solution)/shard_map/dot_general | solution.py:74
  (3 shorter events, 0.0 us)
Async XLA Ops:
  6.5 61.4 %all-gather.4.cloned.1.call-start = ((), (), s32[]{:S(2)}) async-start(), calls=%async_computation.1 | async-start | bytes 6684672 | tf_op jit(solution)/shard_map/all_gather | solution.py:22
  8.4 129.2 %all-gather.8.cloned.1.call-start = ((), (), s32[]{:S(2)}) async-start(), calls=%async_computation.3 | async-start | bytes 2228224 | tf_op jit(solution)/shard_map/all_gather | solution.py:72
  9.1 13.1 %copy-start.4 = (s32[16]{0:T(128)S(1)}, s32[16]{0:T(128)}, u32[]{:S(2)}) copy-start(s32[16]{0:T(128)} %param.9) | copy-start | bytes 196
  22.2 18.9 %copy-start.3 = (bf16[512,128]{1,0:T(8,128)(2,1)S(1)}, bf16[512,128]{1,0:T(8,128)(2,1)}, u32[]{:S(2)}) copy-start(bf16[512,128]{1,0:T(8,128)(2,1)} %param.13) | copy-start | bytes 393220
  31.0 5.9 %copy-start = (bf16[16,256,2048]{2,1,0:T(8,128)(2,1)}, bf16[16,256,2048]{2,1,0:T(8,128)(2,1)S(1)}, u32[]{:S(2)}) copy-start(bf16[16,256,2048]{2,1,0:T(8,128)(2,1)S(1)} %broadcast_select_fusion) | copy-start | bytes 50331652
  37.0 24.5 %collective-permute-start = (bf16[256,2048]{1,0:T(8,128)(2,1)S(1)}, bf16[256,2048]{1,0:T(8,128)(2,1)S(1)}, u32[]{:S(2)}, u32[]{:S(2)}) collective-permute-start(bf16[256,2048]{1,0:T(8,128)(2,1)S(1)} %slice_bitcast_fusion), channel_id=1, source_target_pairs={{0,8},{8,16},{16,24},{24,32},{32,40},{40,48},{48,56},{56,64},{64,7... | collective-permute-start | bytes 3145736 | tf_op jit(solution)/shard_map/ppermute | solution.py:13
  41.9 160.2 %all-gather.6.cloned.1.call-start = ((), (), s32[]{:S(2)}) async-start(), calls=%async_computation.2 | async-start | bytes 5242880 | tf_op jit(solution)/shard_map/all_gather | solution.py:71
  42.0 2.3 %copy-start.1 = (bf16[1024,2048]{1,0:T(8,128)(2,1)S(1)}, bf16[1024,2048]{1,0:T(8,128)(2,1)}, u32[]{:S(2)}) copy-start(bf16[1024,2048]{1,0:T(8,128)(2,1)} %param.7) | copy-start | bytes 12582916
  42.0 19.5 %slice-start = ((bf16[16,256,2048]{2,1,0:T(8,128)(2,1)}), bf16[15,256,2048]{2,1,0:T(8,128)(2,1)S(1)}, s32[]{:S(2)}) async-start(bf16[16,256,2048]{2,1,0:T(8,128)(2,1)} %copy-done), calls=%async_computation.4 | async-start | bytes 31457280 | tf_op jit(solution)/shard_map/slice | solution.py:55
  120.0 2.0 copy-start.2
Sparse Core Ops, SparseCore 0:
  9.0 46.2 all-gather.3
  57.0 37.4 all-gather.7
  137.7 64.4 all-gather.5
where the time goes:
time: 216 us; the launch traced here: 215 us
  matrix products  55.9 us (26%)
  waiting for transfers between devices  42.7 us (20%)
  local copies, waits for them, and re-layouts  42.7 us (20%)
  blocking collectives  35.9 us (17%)
  other arithmetic  20.2 us (9%)
  between operations  13.2 us (6%)
  starting transfers between devices  4.22 us (2%)
    all_to_all x1, blocking collectives, local(): lax.all_to_all(wide_rows, 'head', split_axis=1, concat_axis=0, tiled=True)  35.9 us
    dot_general x3, matrix products, fold_rows(): return jnp.dot(source, shard_rows, preferred_element_type=jnp.float32)  34.1 us
    all_gather x1, waiting for transfers between devices, local(): every_head = lax.all_gather(attended, 'head', axis=1, tiled=True)  26.3 us
    ppermute x1, waiting for transfers between devices, passed_along(): return lax.ppermute(block, axis, route)  16.4 us
    gather x1, local copies, waits for them, and re-layouts, local(): retrieved = jnp.take(neighbor_bank, slots, axis=0)  13.1 us
    unnamed x12, local copies, waits for them, and re-layouts  12.1 us
    dot_general x1, matrix products, attend(): jnp.einsum('chmn,cnhd->cmhd', weights, value_blocks, preferred_element_ty...  11.9 us
    select_n x2, other arithmetic, local(): retrieved = jnp.take(neighbor_bank, slots, axis=0)  9.4 us
  transfers between devices with their start and end apart: 4, of which 2 were waited for; matrix products, arithmetic and copies ran while one was open for 47% of the time, Pallas kernels for 0%

commit v1 on v0

--- a/solution.py
+++ b/solution.py
@@ -5,6 +5,12 @@
 from jax.sharding import PartitionSpec as P
 
 HEAD_DIM = 128
+
+
+def gather_from_all(x, axis, dim):
+    size = lax.axis_size(axis)
+    repeats = [size if d == dim else 1 for d in range(x.ndim)]
+    return lax.all_to_all(jnp.tile(x, repeats), axis, split_axis=dim, concat_axis=dim, tiled=True)
 
 
 def passed_along(block, axis, distance):
@@ -68,7 +74,7 @@
         block_count, neighbor_rows, local_heads, HEAD_DIM
     )
     attended = attend(query_blocks, key_blocks, value_blocks)
-    every_head = lax.all_gather(attended, "head", axis=1, tiled=True)
+    every_head = gather_from_all(attended, "head", 1)
     wide_rows = lax.all_gather(w_out, "seq", axis=1, tiled=True)
     own_columns = lax.all_to_all(wide_rows, "head", split_axis=1, concat_axis=0, tiled=True)
     return jnp.dot(every_head, own_columns, preferred_element_type=jnp.float32).astype(jnp.bfloat16)

time: 216 us -> 224 us (1.037)
  blocking collectives: 35.9 us -> 51.8 us
  waiting for transfers between devices: 42.7 us -> 35.5 us
  starting transfers between devices: 4.22 us -> 8.52 us
  local copies, waits for them, and re-layouts: 42.7 us -> 39.5 us
  matrix products: 55.9 us -> 52.8 us
    all_gather x1 -> x0, waiting for transfers between devices: 26.3 us -> none  [local(): every_head = lax.all_gather(attended, 'head', axis=1, tiled=True)]
    all_gather x1, waiting for transfers between devices: 0.01 us -> 25.1 us  [side_by_side(): lax.all_gather(both, axis, axis=dim, tiled=True)]
    all_to_all x1, blocking collectives: 35.9 us -> 51.8 us  [gather_from_all(): lax.all_to_all(jnp.tile(x, repeats), axis, split_axis=dim, concat_axis=di...]
    unnamed x12 -> x10, local copies, waits for them, and re-layouts: 12.1 us -> 3.82 us
    ppermute x1, waiting for transfers between devices: 16.4 us -> 10.4 us  [passed_along(): return lax.ppermute(block, axis, route)]
    all_to_all x0 -> x1, starting transfers between devices: none -> 4.17 us  [local(): lax.all_to_all(wide_rows, 'head', split_axis=1, concat_axis=0, tiled=True)]
    dot_general x1, matrix products: 6.16 us -> 3.29 us  [local(): jnp.dot(every_head, own_columns, preferred_element_type=jnp.float32)]
where the time goes in v1:
time: 224 us; the launch traced here: 222 us
  matrix products  52.8 us (24%)
  blocking collectives  51.8 us (23%)
  local copies, waits for them, and re-layouts  39.5 us (18%)
  waiting for transfers between devices  35.5 us (16%)
  other arithmetic  20.1 us (9%)
  between operations  13.5 us (6%)
  starting transfers between devices  8.52 us (4%)
    all_to_all x1, blocking collectives, gather_from_all(): lax.all_to_all(jnp.tile(x, repeats), axis, split_axis=dim, concat_axis=di...  51.8 us
    dot_general x3, matrix products, fold_rows(): return jnp.dot(source, shard_rows, preferred_element_type=jnp.float32)  33.8 us
    all_gather x1, waiting for transfers between devices, side_by_side(): lax.all_gather(both, axis, axis=dim, tiled=True)  25.1 us
    gather x1, local copies, waits for them, and re-layouts, local(): retrieved = jnp.take(neighbor_bank, slots, axis=0)  13.1 us
    dot_general x1, matrix products, attend(): jnp.einsum('chmn,cnhd->cmhd', weights, value_blocks, preferred_element_ty...  11.9 us
    ppermute x1, waiting for transfers between devices, passed_along(): return lax.ppermute(block, axis, route)  10.4 us
    select_n x2, other arithmetic, local(): retrieved = jnp.take(neighbor_bank, slots, axis=0)  9.33 us
    reshape x1, local copies, waits for them, and re-layouts, local(): key_sum.astype(jnp.bfloat16)  6.94 us
  transfers between devices with their start and end apart: 4, of which 2 were waited for; matrix products, arithmetic and copies ran while one was open for 47% of the time, Pallas kernels for 0%

profile of v1, /device:TPU:3, one launch (start us, length us, event | category | flops | bytes accessed | tf_op | source)
XLA Modules:
  0.0 221.9 jit_solution(3954884274622827346)
XLA Ops:
  6.5 0.0 all-gather.5.cloned.1.call-start
  6.5 1.7 copy.15
  8.2 0.0 all-gather.5.cloned.1.call-update
  8.2 0.0 all-gather.3.cloned.1.call-start
  8.3 1.8 pad_maximum_fusion.1
  10.1 0.0 all-gather.3.cloned.1.call-update
  10.1 0.7 compare_select_fusion
  10.8 0.0 copy-start.3
  10.8 13.1 %gather_fusion = bf16[16,256,2048]{2,1,0:T(8,128)(2,1)} fusion(bf16[16,256,2048]{2,1,0:T(8,128)(2,1)} %param.8, s32[1024]{0:T(1024)S(1)} %pad_clamp_fusion), kind=kCustom, calls=%fused_computation | custom fusion | bytes 33554496 | tf_op jit(solution)/shard_map/jit(_take)/gather | solution.py:59
  23.9 0.0 copy-done.3
  23.9 8.7 %broadcast_select_fusion = bf16[16,256,2048]{2,1,0:T(8,128)(2,1)S(1)} fusion(bf16[16,256,2048]{2,1,0:T(8,128)(2,1)} %gather_fusion, pred[16]{0:T(512)(128)(4,1)S(1)} %compare_and_fusion), kind=kLoop, calls=%fused_computation.3 | loop fusion | flops 8388608 | bytes 33554448 | tf_op jit(solution)/shard_map/jit(_take)/select_n | solution.py:59
  32.6 0.1 slice_bitcast_fusion
  32.7 0.0 copy-start
  32.7 4.3 %collective-permute-start = (bf16[256,2048]{1,0:T(8,128)(2,1)S(1)}, bf16[256,2048]{1,0:T(8,128)(2,1)S(1)}, u32[]{:S(2)}, u32[]{:S(2)}) collective-permute-start(bf16[256,2048]{1,0:T(8,128)(2,1)S(1)} %slice_bitcast_fusion), channel_id=1, source_target_pairs={{0,8},{8,16},{16,24},{24,32},{32,40},{40,48},{48,56},{56,64},{64,7... | collective-permute-start | bytes 3145736 | tf_op jit(solution)/shard_map/ppermute | solution.py:19
  37.0 1.8 slice.11
  38.9 0.0 copy-done
  38.9 0.9 fusion.1
  39.8 10.4 %collective-permute-done = bf16[256,2048]{1,0:T(8,128)(2,1)S(1)} collective-permute-done((bf16[256,2048]{1,0:T(8,128)(2,1)S(1)}, bf16[256,2048]{1,0:T(8,128)(2,1)S(1)}, u32[]{:S(2)}, u32[]{:S(2)}) %collective-permute-start) | collective-permute-done | bytes 1048608 | tf_op jit(solution)/shard_map/ppermute | solution.py:19
  50.2 6.5 %pad_maximum_fusion = bf16[16,256,2048]{2,1,0:T(8,128)(2,1)} fusion(bf16[15,256,2048]{2,1,0:T(8,128)(2,1)S(1)} %slice.11, bf16[1,256,2048]{2,1,0:T(8,128)(2,1)S(1)} %bitcast.27), kind=kLoop, calls=%fused_computation.2 | loop fusion | flops 8388608 | bytes 33554432 | tf_op jit(solution)/shard_map/concatenate | solution.py:61
  56.6 0.0 all-gather.5.cloned.1.call-done
  56.6 4.2 %copy.16 = bf16[512,4,512]{2,0,1:T(8,128)(2,1)} copy(bf16[512,4,512]{0,2,1:T(8,128)(2,1)} %bitcast.26) | data formatting | bytes 4194304 | tf_op jit(solution)/shard_map/all_to_all | solution.py:79
  60.9 4.2 %all-to-all-start.1 = ((bf16[512,4,512]{2,0,1:T(8,128)(2,1)}), bf16[512,4,512]{2,0,1:T(8,128)(2,1)S(1)}, u32[]{:S(2)}, u32[]{:S(2)}) async-start(bf16[512,4,512]{2,0,1:T(8,128)(2,1)} %copy.16), calls=%async_computation.1 | async-start | bytes 4194304 | tf_op jit(solution)/shard_map/all_to_all | solution.py:79
  65.0 25.1 %all-gather.3.cloned.1.call-done = bf16[2048,1536]{1,0:T(8,128)(2,1)} async-done(((bf16[128,1536]{1,0:T(8,128)(2,1)}), bf16[2048,1536]{1,0:T(8,128)(2,1)}) %all-gather.3.cloned.1.call-update) | async-done | bytes 6291472 | tf_op jit(solution)/shard_map/all_gather | solution.py:28
  90.2 14.4 %convolution_convert_fusion = bf16[4096,512]{1,0:T(8,128)(2,1)} fusion(bf16[4096,2048]{1,0:T(8,128)(2,1)} %bitcast.22, bf16[2048,1536]{1,0:T(8,128)(2,1)} %all-gather.3.cloned.1.call-done), kind=kOutput, calls=%fused_computation.8 | convolution fusion | flops 8592031744 | bytes 23068672 | tf_op jit(solution)/shard_map/dot_general | solution.py:45
  104.6 6.9 %reshape.40 = bf16[16,256,4,128]{3,2,1,0:T(4,128)(2,1)} reshape(bf16[4096,512]{1,0:T(8,128)(2,1)} %convolution_convert_fusion) | data formatting | bytes 8388608 | tf_op jit(solution)/shard_map/reshape | solution.py:70
  111.5 0.0 copy-start.1
  111.5 14.5 %convolution_convert_fusion.1 = bf16[4096,512]{1,0:T(8,128)(2,1)} fusion(bf16[4096,2048]{1,0:T(8,128)(2,1)} %bitcast.23, bf16[2048,1536]{1,0:T(8,128)(2,1)} %all-gather.3.cloned.1.call-done), kind=kOutput, calls=%fused_computation.9 | convolution fusion | flops 8592031744 | bytes 23068672 | tf_op jit(solution)/shard_map/dot_general | solution.py:45
  126.0 0.0 copy-done.1
  126.0 4.9 %fusion.23 = bf16[1024,512]{1,0:T(8,128)(2,1)} fusion(bf16[2048,1536]{1,0:T(8,128)(2,1)} %all-gather.3.cloned.1.call-done, bf16[1024,2048]{1,0:T(8,128)(2,1)S(1)} %copy-done.1, f32[1024]{0:T(1024)S(1)} %add_rsqrt_fusion), kind=kOutput, calls=%fused_computation.29 | convolution fusion | flops 2154299392 | bytes 7344128 | tf_op jit(solution)/shard_map/dot_general | solution.py:45
  131.0 1.3 reshape.39
  132.3 6.9 %reshape.38 = bf16[16,256,4,128]{3,2,1,0:T(4,128)(2,1)} reshape(bf16[4096,512]{1,0:T(8,128)(2,1)} %convolution_convert_fusion.1) | data formatting | bytes 8388608 | tf_op jit(solution)/shard_map/reshape | solution.py:73
  139.2 3.8 %fusion.7 = f32[16,4,64,256]{3,2,1,0:T(8,128)S(1)} fusion(bf16[16,256,4,128]{3,2,1,0:T(4,128)(2,1)} %reshape.40, bf16[16,64,4,128]{3,2,1,0:T(4,128)(2,1)S(1)} %reshape.39), kind=kOutput, calls=%fused_computation.13 | convolution fusion | flops 268435456 | bytes 9437184 | tf_op jit(solution)/shard_map/cmhd,cnhd->chmn/dot_general | solution.py:32
  143.0 0.0 copy-start.2
  143.0 2.0 copy-done.2
  144.9 1.6 fusion.42
  146.6 11.9 %fusion.30 = bf16[16,64,4,128]{3,1,2,0:T(8,128)(2,1)S(1)} fusion(bf16[16,256,4,128]{3,2,1,0:T(4,128)(2,1)} %reshape.38, f32[16,4,64]{2,1,0:T(4,128)S(1)} %fusion.42, f32[16,4,64,256]{3,2,1,0:T(8,128)} %copy-done.2), kind=kOutput, calls=%fused_computation.30 | convolution fusion | flops 274206976 | bytes 9453568 | tf_op jit(solution)/shard_map/chmn,cnhd->cmhd/dot_general | solution.py:38
  158.5 0.9 copy.14
  159.4 0.2 copy.29
  159.6 0.0 all-to-all-done.1
  159.6 0.3 tile.9
  159.9 51.8 %all_to_all.22 = bf16[1024,4,512]{2,0,1:T(8,128)(2,1)S(1)} all-to-all(bf16[1024,4,512]{2,0,1:T(8,128)(2,1)S(1)} %tile.9), channel_id=1, replica_groups=mesh['seq'=16,'head'=4,'batch'=2] {'head'}, dimensions={1} | all-to-all | bytes 8388608 | tf_op jit(solution)/shard_map/all_to_all | solution.py:13
  211.7 3.3 %bitcast_convert_fusion = bf16[1024,512]{1,0:T(8,128)(2,1)} fusion(bf16[1024,4,512]{2,0,1:T(8,128)(2,1)S(1)} %all_to_all.22, bf16[512,4,512]{2,0,1:T(8,128)(2,1)S(1)} %all-to-all-done.1), kind=kOutput, calls=%fused_computation.23 | convolution fusion | flops 2148007936 | bytes 7340032 | tf_op jit(solution)/shard_map/dot_general | solution.py:80
  (3 shorter events, 0.0 us)
Async XLA Ops:
  6.5 50.1 %all-gather.5.cloned.1.call-start = ((), (), s32[]{:S(2)}) async-start(), calls=%async_computation.3 | async-start | bytes 2228224 | tf_op jit(solution)/shard_map/all_gather | solution.py:78
  8.2 82.0 %all-gather.3.cloned.1.call-start = ((), (), s32[]{:S(2)}) async-start(), calls=%async_computation.2 | async-start | bytes 6684672 | tf_op jit(solution)/shard_map/all_gather | solution.py:28
  10.8 13.1 %copy-start.3 = (s32[16]{0:T(128)S(1)}, s32[16]{0:T(128)}, u32[]{:S(2)}) copy-start(s32[16]{0:T(128)} %param.9) | copy-start | bytes 196
  32.7 6.2 %copy-start = (bf16[1024,2048]{1,0:T(8,128)(2,1)S(1)}, bf16[1024,2048]{1,0:T(8,128)(2,1)}, u32[]{:S(2)}) copy-start(bf16[1024,2048]{1,0:T(8,128)(2,1)} %param.7) | copy-start | bytes 12582916
  32.7 17.4 %collective-permute-start = (bf16[256,2048]{1,0:T(8,128)(2,1)S(1)}, bf16[256,2048]{1,0:T(8,128)(2,1)S(1)}, u32[]{:S(2)}, u32[]{:S(2)}) collective-permute-start(bf16[256,2048]{1,0:T(8,128)(2,1)S(1)} %slice_bitcast_fusion), channel_id=1, source_target_pairs={{0,8},{8,16},{16,24},{24,32},{32,40},{40,48},{48,56},{56,64},{64,7... | collective-permute-start | bytes 3145736 | tf_op jit(solution)/shard_map/ppermute | solution.py:19
  60.9 98.7 %all-to-all-start.1 = ((bf16[512,4,512]{2,0,1:T(8,128)(2,1)}), bf16[512,4,512]{2,0,1:T(8,128)(2,1)S(1)}, u32[]{:S(2)}, u32[]{:S(2)}) async-start(bf16[512,4,512]{2,0,1:T(8,128)(2,1)} %copy.16), calls=%async_computation.1 | async-start | bytes 4194304 | tf_op jit(solution)/shard_map/all_to_all | solution.py:79
  111.5 14.5 %copy-start.1 = (bf16[1024,2048]{1,0:T(8,128)(2,1)S(1)}, bf16[1024,2048]{1,0:T(8,128)(2,1)}, u32[]{:S(2)}) copy-start(bf16[1024,2048]{1,0:T(8,128)(2,1)} %param.7) | copy-start | bytes 12582916
  143.0 2.0 copy-start.2
Sparse Core Ops, SparseCore 0:
  9.0 36.7 all-gather.4
  47.6 42.5 all-gather.2
